TPU v7x, 32 devices: a whole 2x2x4 slice. The times are simulated.
32 devices in a mesh: kx: 4 (over y, x), ky: 8 (over z, core).
Axes of the slice: x: 2, y: 2, z: 4, core: 2. Of those that a mesh axis runs over, the one named last changes fastest.
Arguments:
- wannier: bfloat16 [16, 64, 64, 128], P('kx', 'ky'), may hold values from -0.5 to 0.5
- coupling: bfloat16 [3, 16, 64, 6, 64, 128], P(None, 'kx', 'ky'), may hold values from -6 to 6
- kq_map: int32 [3, 1024], replicated, may hold values from 0 to 1023, as said below
Outputs:
- rotated: bfloat16 [3, 16, 64, 6, 64, 128], P(None, 'kx', 'ky')
Inputs may be any that keep to these rules, and one draw needn't show every extreme that they name: For every q there are offsets a and b with kq_map[q, x * 64 + y] = ((x + a) mod 16) * 64 + (y + b) mod 64.
All inputs are finite; a program needn't handle non-finite values.
Results may differ from a plain program's by a relative error of at most 0.0049.
Values may be sent and summed in bfloat16 or wider, within the bound.
A program may use at most 192 MiB of HBM per device.

v0:
```python
import functools
import math

import jax
import jax.numpy as jnp
from jax import lax
from jax.experimental import pallas as pl
from jax.sharding import PartitionSpec as P


def rotate_kernel(coupling_ref, wannier_ref, *refs):
    partner_refs, out_ref = refs[:-1], refs[-1]
    qpoints, points, modes, bands, width = coupling_ref.shape
    half = width // 2

    def rotate_point(point, carry):
        real = wannier_ref[point, :, :half]
        imag = wannier_ref[point, :, half:]
        factor = jnp.concatenate(
            [jnp.concatenate([real, imag], axis=1), jnp.concatenate([-imag, real], axis=1)], axis=0
        )
        blank = jnp.zeros_like(factor)
        pair_factor = jnp.concatenate(
            [jnp.concatenate([factor, blank], axis=1), jnp.concatenate([blank, factor], axis=1)], axis=0
        )
        blocks = coupling_ref[:, point].reshape(qpoints * modes // 2, 2, bands, width)
        pairs = jnp.concatenate(
            [blocks[:, 0].reshape(-1, width), blocks[:, 1].reshape(-1, width)], axis=1
        )
        turned = jnp.dot(pairs, pair_factor, preferred_element_type=jnp.float32).astype(jnp.bfloat16)
        for qpoint in range(qpoints):
            stacked = []
            for mode in range(modes):
                row, side = divmod(qpoint * modes + mode, 2)
                own = turned[row * bands : (row + 1) * bands, side * width : (side + 1) * width]
                swapped = jnp.concatenate([own[:, half:], -own[:, :half]], axis=1)
                stacked.append(jnp.concatenate([own, swapped], axis=0))
            partner = partner_refs[qpoint][point]
            partner_rows = jnp.concatenate([partner[:, :half], partner[:, half:]], axis=0)
            rotated = lax.dot_general(
                partner_rows,
                jnp.concatenate(stacked, axis=1),
                (((0,), (0,)), ((), ())),
                preferred_element_type=jnp.float32,
            ).astype(jnp.bfloat16)
            for mode in range(modes):
                out_ref[qpoint, point, mode] = rotated[:, mode * width : (mode + 1) * width]
        return carry

    lax.fori_loop(0, points, rotate_point, 0, unroll=points)


def rotate(coupling, wannier, partners, tile):
    qpoints, points, modes, bands, width = coupling.shape
    one_point = pl.BlockSpec((tile, bands, width), lambda i: (i, 0, 0))
    all_modes = pl.BlockSpec((qpoints, tile, modes, bands, width), lambda i: (0, i, 0, 0, 0))
    return pl.pallas_call(
        rotate_kernel,
        grid=(points // tile,),
        in_specs=[all_modes, one_point] + [one_point] * len(partners),
        out_specs=all_modes,
        out_shape=jax.ShapeDtypeStruct(coupling.shape, jnp.bfloat16),
    )(coupling, wannier, *partners)


def shift_blocks(block, shift_x, shift_y):
    count_x = lax.axis_size("kx")
    count_y = lax.axis_size("ky")
    pairs = [
        (((x + shift_x) % count_x) * count_y + (y + shift_y) % count_y, x * count_y + y)
        for x in range(count_x)
        for y in range(count_y)
    ]
    return lax.ppermute(block, ("kx", "ky"), pairs)


def shift_rows(block, offset_x):
    shift_x, inner_x = divmod(offset_x, block.shape[0])
    near = shift_blocks(block[inner_x:], shift_x, 0)
    if inner_x == 0:
        return near
    far = shift_blocks(block[:inner_x], shift_x + 1, 0)
    return jnp.concatenate([near, far], axis=0)


def per_device(wannier, coupling, kq_map):
    rows_x, cols_y, bands, width = wannier.shape
    count_y = lax.axis_size("ky")
    total_x = rows_x * lax.axis_size("kx")
    total_y = cols_y * count_y
    qpoints, modes = coupling.shape[0], coupling.shape[3]
    points = rows_x * cols_y
    columns = jnp.concatenate([wannier, shift_blocks(wannier, 0, 1)], axis=1)
    along_y = [functools.partial(shift_blocks, shift_x=0, shift_y=y) for y in range(count_y)]
    along_x = [functools.partial(shift_rows, offset_x=x) for x in range(total_x)]
    partners = []
    for qpoint in range(qpoints):
        offset_x, offset_y = kq_map[qpoint, 0] // total_y, kq_map[qpoint, 0] % total_y
        aligned = lax.dynamic_slice_in_dim(columns, offset_y % cols_y, cols_y, axis=1)
        aligned = lax.switch(offset_y // cols_y, along_y, aligned)
        partner = lax.switch(offset_x, along_x, aligned)
        partners.append(partner.reshape(points, bands, width))
    rotated = rotate(
        coupling.reshape(qpoints, points, modes, bands, width),
        wannier.reshape(points, bands, width),
        partners,
        math.gcd(points, 4),
    )
    return rotated.reshape(coupling.shape)


def solution(mesh):
    in_specs = (P("kx", "ky", None, None), P(None, "kx", "ky", None, None, None), P())
    out_specs = P(None, "kx", "ky", None, None, None)
    return jax.shard_map(
        per_device, mesh=mesh, in_specs=in_specs, out_specs=out_specs, check_vma=False
    )
```

profile of v0, /device:TPU:0, one launch (start us, length us, event | category | flops | bytes accessed | tf_op | source)
XLA Modules:
  0.0 110.6 jit_solution(8525138983299096024)
XLA Ops:
  0.0 4.5 %collective-permute-start.108 = (bf16[4,8,64,128]{3,2,1,0:T(8,128)(2,1)}, bf16[4,8,64,128]{3,2,1,0:T(8,128)(2,1)S(1)}, u32[]{:S(2)}, u32[]{:S(2)}) collective-permute-start(bf16[4,8,64,128]{3,2,1,0:T(8,128)(2,1)} %param.75), channel_id=1, source_target_pairs={{1,0},{2,1},{3,2},{4,3},{5,4},{6,5},{7,6},{0,7},{9,8},{10,9},{11,1... | collective-permute-start | bytes 1572872 | tf_op jit(solution)/shard_map/ppermute | solution.py:74
  4.5 1.3 %fusion.12 = (s32[1,1]{1,0:T(1,128)}, s32[1,1]{1,0:T(1,128)}, s32[1,1]{1,0:T(1,128)}) fusion(s32[3,1024]{1,0:T(4,128)} %param.77), kind=kLoop, calls=%fused_computation.53 | loop fusion | bytes 24 | tf_op jit(solution)/shard_map/slice | solution.py:98
  13.5 1.1 constant_dynamic-update-slice_fusion.1
  14.6 0.0 collective-permute-done.108
  14.6 0.1 constant_dynamic-update-slice_fusion
  14.7 0.1 constant_dynamic-slice_fusion
  14.9 10.6 %conditional.10 = (bf16[4,8,64,128]{3,2,1,0:T(8,128)(2,1)}) conditional(s32[]{:T(128)} %clamp.23, bf16[4,8,64,128]{3,2,1,0:T(8,128)(2,1)S(1)} %get-tuple-element.182, bf16[4,8,64,128]{3,2,1,0:T(8,128)(2,1)S(1)} %get-tuple-element.182, bf16[4,8,64,128]{3,2,1,0:T(8,128)(2,1)S(1)} %get-tuple-element.182, ...), branch_computations={%region_48.49_spmd, %region_49.50_spmd, %region_50.51_spmd, %regio... | conditional | bytes 2097200 | solution.py:100
  14.9 0.1 collective-permute-start.31
  15.0 10.5 %collective-permute-done.31 = bf16[4,8,64,128]{3,2,1,0:T(8,128)(2,1)} collective-permute-done((bf16[4,8,64,128]{3,2,1,0:T(8,128)(2,1)S(1)}, bf16[4,8,64,128]{3,2,1,0:T(8,128)(2,1)}, u32[]{:S(2)}, u32[]{:S(2)}) %collective-permute-start.31) | collective-permute-done | bytes 524320 | tf_op jit(solution)/shard_map/cond/branch_7_fun/ppermute | solution.py:74
  25.4 11.1 %conditional.11 = (bf16[32,64,128]{2,1,0:T(8,128)(2,1)}) conditional(s32[]{:T(128)} %clamp.22, bf16[4,8,64,128]{3,2,1,0:T(8,128)(2,1)} %get-tuple-element.192, bf16[4,8,64,128]{3,2,1,0:T(8,128)(2,1)} %get-tuple-element.192, bf16[4,8,64,128]{3,2,1,0:T(8,128)(2,1)} %get-tuple-element.192, ...), branch_computations={%region_56.57_spmd, %region_57.58_spmd, %region_58.59_spmd, %regio... | conditional | flops 262144 | bytes 4194392 | solution.py:101
  25.4 1.0 slice.213
  26.5 1.6 %collective-permute-start.76 = (bf16[3,8,64,128]{3,2,1,0:T(8,128)(2,1)S(1)}, bf16[3,8,64,128]{3,2,1,0:T(8,128)(2,1)S(1)}, u32[]{:S(2)}, u32[]{:S(2)}) collective-permute-start(bf16[3,8,64,128]{3,2,1,0:T(8,128)(2,1)S(1)} %slice.213), channel_id=1, source_target_pairs={{16,0},{17,1},{18,2},{19,3},{20,4},{21,5},{22,6},{23,7},{24,8},{25... | collective-permute-start | bytes 1179656 | tf_op jit(solution)/shard_map/cond/branch_9_fun/ppermute | solution.py:74
  28.1 0.9 slice.214
  29.0 1.5 %collective-permute-start.77 = (bf16[1,8,64,128]{3,2,1,0:T(8,128)(2,1)S(1)}, bf16[1,8,64,128]{3,2,1,0:T(8,128)(2,1)S(1)}, u32[]{:S(2)}, u32[]{:S(2)}) collective-permute-start(bf16[1,8,64,128]{3,2,1,0:T(8,128)(2,1)S(1)} %slice.214), channel_id=1, source_target_pairs={{24,0},{25,1},{26,2},{27,3},{28,4},{29,5},{30,6},{31,7},{0,8},{1,9... | collective-permute-start | bytes 393224 | tf_op jit(solution)/shard_map/cond/branch_9_fun/ppermute | solution.py:74
  30.5 4.5 %collective-permute-done.77 = bf16[1,8,64,128]{3,2,1,0:T(8,128)(2,1)S(1)} collective-permute-done((bf16[1,8,64,128]{3,2,1,0:T(8,128)(2,1)S(1)}, bf16[1,8,64,128]{3,2,1,0:T(8,128)(2,1)S(1)}, u32[]{:S(2)}, u32[]{:S(2)}) %collective-permute-start.77) | collective-permute-done | bytes 131104 | tf_op jit(solution)/shard_map/cond/branch_9_fun/ppermute | solution.py:74
  35.0 0.7 collective-permute-done.76
  35.7 0.9 pad_maximum_fusion.30
  36.6 23.2 %conditional.8 = (bf16[4,8,64,128]{3,2,1,0:T(8,128)(2,1)}) conditional(s32[]{:T(128)} %clamp.21, bf16[4,8,64,128]{3,2,1,0:T(8,128)(2,1)S(1)} %get-tuple-element.183, bf16[4,8,64,128]{3,2,1,0:T(8,128)(2,1)S(1)} %get-tuple-element.183, bf16[4,8,64,128]{3,2,1,0:T(8,128)(2,1)S(1)} %get-tuple-element.183, ...), branch_computations={%region_24.25_spmd, %region_25.26_spmd, %region_26.27_spmd, %regio... | conditional | bytes 2097200 | solution.py:100
  36.6 1.5 %collective-permute-start.16 = (bf16[4,8,64,128]{3,2,1,0:T(8,128)(2,1)S(1)}, bf16[4,8,64,128]{3,2,1,0:T(8,128)(2,1)}, u32[]{:S(2)}, u32[]{:S(2)}) collective-permute-start(bf16[4,8,64,128]{3,2,1,0:T(8,128)(2,1)S(1)} %param.28), channel_id=1, source_target_pairs={{4,0},{5,1},{6,2},{7,3},{0,4},{1,5},{2,6},{3,7},{12,8},{13,9},{14,... | collective-permute-start | bytes 1572872 | tf_op jit(solution)/shard_map/cond/branch_4_fun/ppermute | solution.py:74
  38.1 21.7 %collective-permute-done.16 = bf16[4,8,64,128]{3,2,1,0:T(8,128)(2,1)} collective-permute-done((bf16[4,8,64,128]{3,2,1,0:T(8,128)(2,1)S(1)}, bf16[4,8,64,128]{3,2,1,0:T(8,128)(2,1)}, u32[]{:S(2)}, u32[]{:S(2)}) %collective-permute-start.16) | collective-permute-done | bytes 524320 | tf_op jit(solution)/shard_map/cond/branch_4_fun/ppermute | solution.py:74
  59.8 12.9 %conditional.9 = (bf16[32,64,128]{2,1,0:T(8,128)(2,1)}) conditional(s32[]{:T(128)} %clamp.20, bf16[4,8,64,128]{3,2,1,0:T(8,128)(2,1)} %get-tuple-element.190, bf16[4,8,64,128]{3,2,1,0:T(8,128)(2,1)} %get-tuple-element.190, bf16[4,8,64,128]{3,2,1,0:T(8,128)(2,1)} %get-tuple-element.190, ...), branch_computations={%region_32.33_spmd, %region_33.34_spmd, %region_34.35_spmd, %regio... | conditional | flops 262144 | bytes 4194392 | solution.py:101
  59.8 1.0 slice.194
  60.8 0.1 collective-permute-start.63
  60.9 0.9 slice.193
  61.8 1.6 %collective-permute-start.62 = (bf16[1,8,64,128]{3,2,1,0:T(8,128)(2,1)S(1)}, bf16[1,8,64,128]{3,2,1,0:T(8,128)(2,1)S(1)}, u32[]{:S(2)}, u32[]{:S(2)}) collective-permute-start(bf16[1,8,64,128]{3,2,1,0:T(8,128)(2,1)S(1)} %slice.193), channel_id=1, source_target_pairs={{16,0},{17,1},{18,2},{19,3},{20,4},{21,5},{22,6},{23,7},{24,8},{25... | collective-permute-start | bytes 393224 | tf_op jit(solution)/shard_map/cond/branch_11_fun/ppermute | solution.py:74
  63.4 8.5 %collective-permute-done.62 = bf16[1,8,64,128]{3,2,1,0:T(8,128)(2,1)S(1)} collective-permute-done((bf16[1,8,64,128]{3,2,1,0:T(8,128)(2,1)S(1)}, bf16[1,8,64,128]{3,2,1,0:T(8,128)(2,1)S(1)}, u32[]{:S(2)}, u32[]{:S(2)}) %collective-permute-start.62) | collective-permute-done | bytes 131104 | tf_op jit(solution)/shard_map/cond/branch_11_fun/ppermute | solution.py:74
  71.8 0.0 collective-permute-done.63
  71.8 0.8 pad_maximum_fusion.20
  72.7 13.9 %conditional.6 = (bf16[4,8,64,128]{3,2,1,0:T(8,128)(2,1)}) conditional(s32[]{:T(128)} %clamp.19, bf16[4,8,64,128]{3,2,1,0:T(8,128)(2,1)S(1)} %get-tuple-element.184, bf16[4,8,64,128]{3,2,1,0:T(8,128)(2,1)S(1)} %get-tuple-element.184, bf16[4,8,64,128]{3,2,1,0:T(8,128)(2,1)S(1)} %get-tuple-element.184, ...), branch_computations={%region_0.1_spmd, %region_1.2_spmd, %region_2.3_spmd, %region_3.4_... | conditional | bytes 2097200 | solution.py:100
  72.7 0.0 collective-permute-start.7
  72.7 13.9 %collective-permute-done.7 = bf16[4,8,64,128]{3,2,1,0:T(8,128)(2,1)} collective-permute-done((bf16[4,8,64,128]{3,2,1,0:T(8,128)(2,1)S(1)}, bf16[4,8,64,128]{3,2,1,0:T(8,128)(2,1)}, u32[]{:S(2)}, u32[]{:S(2)}) %collective-permute-start.7) | collective-permute-done | bytes 524320 | tf_op jit(solution)/shard_map/cond/branch_7_fun/ppermute | solution.py:74
  86.6 9.2 %conditional.7 = (bf16[32,64,128]{2,1,0:T(8,128)(2,1)}) conditional(s32[]{:T(128)} %clamp.18, bf16[4,8,64,128]{3,2,1,0:T(8,128)(2,1)} %get-tuple-element.188, bf16[4,8,64,128]{3,2,1,0:T(8,128)(2,1)} %get-tuple-element.188, bf16[4,8,64,128]{3,2,1,0:T(8,128)(2,1)} %get-tuple-element.188, ...), branch_computations={%region_8.9_spmd, %region_9.10_spmd, %region_10.11_spmd, %region_1... | conditional | flops 262144 | bytes 4194392 | solution.py:101
  86.6 1.1 fusion.3
  87.6 0.1 collective-permute-start.90
  87.7 0.0 collective-permute-start.91
  87.7 7.2 %collective-permute-done.90 = bf16[2,8,64,128]{3,2,1,0:T(8,128)(2,1)S(1)} collective-permute-done((bf16[2,8,64,128]{3,2,1,0:T(8,128)(2,1)S(1)}, bf16[2,8,64,128]{3,2,1,0:T(8,128)(2,1)S(1)}, u32[]{:S(2)}, u32[]{:S(2)}) %collective-permute-start.90) | collective-permute-done | bytes 262176 | tf_op jit(solution)/shard_map/cond/branch_14_fun/ppermute | solution.py:74
  95.0 0.0 collective-permute-done.91
  95.0 0.9 pad_maximum_fusion.10
  95.8 14.7 %shard_map.37 = bf16[3,32,6,64,128]{4,3,2,1,0:T(8,128)(2,1)} custom-call(bf16[3,32,6,64,128]{4,3,2,1,0:T(8,128)(2,1)} %bitcast.54, bf16[32,64,128]{2,1,0:T(8,128)(2,1)} %bitcast.55, bf16[32,64,128]{2,1,0:T(8,128)(2,1)} %get-tuple-element.189.refs_0_, bf16[32,64,128]{2,1,0:T(8,128)(2,1)} %get-tuple-element.191.refs_1_, ...), custom_call_target="tpu_custom_call" | custom-call | tf_op jit(solution)/shard_map/pallas_call | solution.py:57
Async XLA Ops:
  0.0 14.6 %collective-permute-start.108 = (bf16[4,8,64,128]{3,2,1,0:T(8,128)(2,1)}, bf16[4,8,64,128]{3,2,1,0:T(8,128)(2,1)S(1)}, u32[]{:S(2)}, u32[]{:S(2)}) collective-permute-start(bf16[4,8,64,128]{3,2,1,0:T(8,128)(2,1)} %param.75), channel_id=1, source_target_pairs={{1,0},{2,1},{3,2},{4,3},{5,4},{6,5},{7,6},{0,7},{9,8},{10,9},{11,1... | collective-permute-start | bytes 1572872 | tf_op jit(solution)/shard_map/ppermute | solution.py:74
  14.9 10.6 %collective-permute-start.31 = (bf16[4,8,64,128]{3,2,1,0:T(8,128)(2,1)S(1)}, bf16[4,8,64,128]{3,2,1,0:T(8,128)(2,1)}, u32[]{:S(2)}, u32[]{:S(2)}) collective-permute-start(bf16[4,8,64,128]{3,2,1,0:T(8,128)(2,1)S(1)} %param.55), channel_id=1, source_target_pairs={{7,0},{0,1},{1,2},{2,3},{3,4},{4,5},{5,6},{6,7},{15,8},{8,9},{9,10... | collective-permute-start | bytes 1572872 | tf_op jit(solution)/shard_map/cond/branch_7_fun/ppermute | solution.py:74
  26.5 9.2 %collective-permute-start.76 = (bf16[3,8,64,128]{3,2,1,0:T(8,128)(2,1)S(1)}, bf16[3,8,64,128]{3,2,1,0:T(8,128)(2,1)S(1)}, u32[]{:S(2)}, u32[]{:S(2)}) collective-permute-start(bf16[3,8,64,128]{3,2,1,0:T(8,128)(2,1)S(1)} %slice.213), channel_id=1, source_target_pairs={{16,0},{17,1},{18,2},{19,3},{20,4},{21,5},{22,6},{23,7},{24,8},{25... | collective-permute-start | bytes 1179656 | tf_op jit(solution)/shard_map/cond/branch_9_fun/ppermute | solution.py:74
  29.0 6.0 %collective-permute-start.77 = (bf16[1,8,64,128]{3,2,1,0:T(8,128)(2,1)S(1)}, bf16[1,8,64,128]{3,2,1,0:T(8,128)(2,1)S(1)}, u32[]{:S(2)}, u32[]{:S(2)}) collective-permute-start(bf16[1,8,64,128]{3,2,1,0:T(8,128)(2,1)S(1)} %slice.214), channel_id=1, source_target_pairs={{24,0},{25,1},{26,2},{27,3},{28,4},{29,5},{30,6},{31,7},{0,8},{1,9... | collective-permute-start | bytes 393224 | tf_op jit(solution)/shard_map/cond/branch_9_fun/ppermute | solution.py:74
  36.6 23.2 %collective-permute-start.16 = (bf16[4,8,64,128]{3,2,1,0:T(8,128)(2,1)S(1)}, bf16[4,8,64,128]{3,2,1,0:T(8,128)(2,1)}, u32[]{:S(2)}, u32[]{:S(2)}) collective-permute-start(bf16[4,8,64,128]{3,2,1,0:T(8,128)(2,1)S(1)} %param.28), channel_id=1, source_target_pairs={{4,0},{5,1},{6,2},{7,3},{0,4},{1,5},{2,6},{3,7},{12,8},{13,9},{14,... | collective-permute-start | bytes 1572872 | tf_op jit(solution)/shard_map/cond/branch_4_fun/ppermute | solution.py:74
  60.8 11.0 %collective-permute-start.63 = (bf16[3,8,64,128]{3,2,1,0:T(8,128)(2,1)S(1)}, bf16[3,8,64,128]{3,2,1,0:T(8,128)(2,1)S(1)}, u32[]{:S(2)}, u32[]{:S(2)}) collective-permute-start(bf16[3,8,64,128]{3,2,1,0:T(8,128)(2,1)S(1)} %slice.194), channel_id=1, source_target_pairs={{24,0},{25,1},{26,2},{27,3},{28,4},{29,5},{30,6},{31,7},{0,8},{1,9... | collective-permute-start | bytes 1179656 | tf_op jit(solution)/shard_map/cond/branch_11_fun/ppermute | solution.py:74
  61.8 10.1 %collective-permute-start.62 = (bf16[1,8,64,128]{3,2,1,0:T(8,128)(2,1)S(1)}, bf16[1,8,64,128]{3,2,1,0:T(8,128)(2,1)S(1)}, u32[]{:S(2)}, u32[]{:S(2)}) collective-permute-start(bf16[1,8,64,128]{3,2,1,0:T(8,128)(2,1)S(1)} %slice.193), channel_id=1, source_target_pairs={{16,0},{17,1},{18,2},{19,3},{20,4},{21,5},{22,6},{23,7},{24,8},{25... | collective-permute-start | bytes 393224 | tf_op jit(solution)/shard_map/cond/branch_11_fun/ppermute | solution.py:74
  72.7 13.9 %collective-permute-start.7 = (bf16[4,8,64,128]{3,2,1,0:T(8,128)(2,1)S(1)}, bf16[4,8,64,128]{3,2,1,0:T(8,128)(2,1)}, u32[]{:S(2)}, u32[]{:S(2)}) collective-permute-start(bf16[4,8,64,128]{3,2,1,0:T(8,128)(2,1)S(1)} %param.7), channel_id=1, source_target_pairs={{7,0},{0,1},{1,2},{2,3},{3,4},{4,5},{5,6},{6,7},{15,8},{8,9},{9,10... | collective-permute-start | bytes 1572872 | tf_op jit(solution)/shard_map/cond/branch_7_fun/ppermute | solution.py:74
  87.6 7.3 %collective-permute-start.90 = (bf16[2,8,64,128]{3,2,1,0:T(8,128)(2,1)S(1)}, bf16[2,8,64,128]{3,2,1,0:T(8,128)(2,1)S(1)}, u32[]{:S(2)}, u32[]{:S(2)}) collective-permute-start(bf16[2,8,64,128]{3,2,1,0:T(8,128)(2,1)S(1)} %get-tuple-element.164), channel_id=1, source_target_pairs={{24,0},{25,1},{26,2},{27,3},{28,4},{29,5},{30,6},{31,7},{0,8},{1,9... | collective-permute-start | bytes 786440 | tf_op jit(solution)/shard_map/cond/branch_14_fun/ppermute | solution.py:74
  87.7 7.3 %collective-permute-start.91 = (bf16[2,8,64,128]{3,2,1,0:T(8,128)(2,1)S(1)}, bf16[2,8,64,128]{3,2,1,0:T(8,128)(2,1)S(1)}, u32[]{:S(2)}, u32[]{:S(2)}) collective-permute-start(bf16[2,8,64,128]{3,2,1,0:T(8,128)(2,1)S(1)} %get-tuple-element.165), channel_id=1, source_target_pairs={{0,0},{1,1},{2,2},{3,3},{4,4},{5,5},{6,6},{7,7},{8,8},{9,9},{10,10... | collective-permute-start | bytes 786440 | tf_op jit(solution)/shard_map/cond/branch_14_fun/ppermute | solution.py:74
where the time goes:
time: 109 us; the launch traced here: 111 us
  waiting for transfers between devices  67 us (61%)
  Pallas kernels  14.7 us (13%)
  starting transfers between devices  10.9 us (10%)
  between operations  7.71 us (7%)
  local copies, waits for them, and re-layouts  7.57 us (7%)
  other arithmetic  2.55 us (2%)
    ppermute x10, waiting for transfers between devices, shift_blocks(): return lax.ppermute(block, ('kx', 'ky'), pairs)  67 us
    pallas_call x1, Pallas kernels, rotate(): pl.pallas_call(rotate_kernel, grid=(points // tile,), in_specs=[all_modes...  14.7 us
    ppermute x10, starting transfers between devices, shift_blocks(): return lax.ppermute(block, ('kx', 'ky'), pairs)  10.9 us
    slice x3, local copies, waits for them, and re-layouts, shift_rows(): near = shift_blocks(block[inner_x:], shift_x, 0)  3 us
    concatenate x3, other arithmetic, shift_rows(): return jnp.concatenate([near, far], axis=0)  2.55 us
  transfers between devices with their start and end apart: 10, of which 7 were waited for; matrix products, arithmetic and copies ran while one was open for 4% of the time, Pallas kernels for 0%

commit v1 on v0

v1 whole, which is shorter than its diff:
```python
import functools

import jax
import jax.numpy as jnp
from jax import lax
from jax.experimental import pallas as pl
from jax.experimental.pallas import tpu as pltpu
from jax.sharding import PartitionSpec as P

MESH = pl.DeviceIdType.MESH
CORES = 2
SLAB = 16


def exchange_kernel(plan, map_ref, wannier_ref, partner_ref, *scratch):
    count_x, planes, rows_x, cols_y, qpoints, parts, waves = plan
    mates = count_x * CORES
    total_x, total_y, blocks = count_x * rows_x, planes * CORES * cols_y, planes * CORES
    gathered, staged = scratch[:waves], scratch[waves : 2 * waves]
    spread_send, spread_recv, spread_self, chain_send, chain_recv, pick_send, pick_recv, pick_self = scratch[2 * waves :]

    here_x, here_y = lax.axis_index("kx"), lax.axis_index("ky")
    plane, core = here_y // CORES, here_y % CORES
    mate = here_x * CORES + core

    def device_of(other):
        return (other // CORES, plane * CORES + other % CORES)

    def part_of(other):
        return other // cols_y if parts > 1 else 0

    def slab(part, wave):
        return pl.ds(pl.multiple_of((part * waves + wave) * SLAB, SLAB), SLAB)

    def spread(wave, step):
        other = (mate + step) % mates
        source = wannier_ref.at[:, other % cols_y, slab(part_of(other), wave), :]
        target = gathered[wave].at[here_y, pl.ds(here_x * rows_x, rows_x)]
        if step == 0:
            return pltpu.make_async_copy(source, target, spread_self.at[wave])
        return pltpu.make_async_remote_copy(
            source, target, spread_send.at[wave, step], spread_recv.at[wave, step], device_of(other), MESH
        )

    def chain(wave, origin, distance, side):
        block = gathered[wave].at[pl.ds(origin * CORES, CORES)]
        target = (here_x, here_y + (CORES if side else -CORES))
        return pltpu.make_async_remote_copy(
            block, block, chain_send.at[wave, distance, side], chain_recv.at[wave, origin], target, MESH
        )

    def pick(wave, step):
        source = staged[wave].at[step]
        target = partner_ref.at[mate % cols_y, :, :, slab(part_of(mate), wave), :]
        if step == 0:
            return pltpu.make_async_copy(source, target, pick_self.at[wave])
        return pltpu.make_async_remote_copy(
            source, target, pick_send.at[wave, step], pick_recv.at[wave, step], device_of((mate + step) % mates), MESH
        )

    def stage(wave):
        kind = mate % cols_y

        def one(step, carry):
            other = (mate + step) % mates
            for q in range(qpoints):
                shift_x, shift_y = map_ref[q, 0] // total_y, map_ref[q, 0] % total_y
                block = (plane * CORES + other % CORES + (shift_y - kind + cols_y - 1) // cols_y) % blocks
                for row in range(rows_x):
                    staged[wave][step, q, row] = gathered[wave][block, (other // CORES * rows_x + shift_x + row) % total_x]
            return carry

        lax.fori_loop(0, mates, one, 0)

    has_left, has_right = plane > 0, plane < planes - 1

    barrier = pltpu.get_barrier_semaphore()
    for step in range(1, mates):
        pl.semaphore_signal(barrier, inc=1, device_id=device_of((mate + step) % mates), device_id_type=MESH)

    @pl.when(has_left)
    def _():
        pl.semaphore_signal(barrier, inc=1, device_id=(here_x, here_y - CORES), device_id_type=MESH)

    @pl.when(has_right)
    def _():
        pl.semaphore_signal(barrier, inc=1, device_id=(here_x, here_y + CORES), device_id_type=MESH)

    pl.semaphore_wait(barrier, mates - 1 + has_left.astype(jnp.int32) + has_right.astype(jnp.int32))

    for wave in range(waves):
        for step in range(mates):
            spread(wave, step).start()

    def send(wave, origin, distance, side):
        @pl.when(has_right if side else has_left)
        def _():
            chain(wave, origin, distance, side).start()

    for tick in range(waves + planes):
        if tick < waves:
            spread(tick, 0).wait()
            for step in range(1, mates):
                spread(tick, step).wait_recv()
            for side in range(2):
                send(tick, plane, 0, side)
        for distance in range(1, planes):
            wave = tick - distance
            if not 0 <= wave < waves:
                continue

            @pl.when(plane + distance < planes)
            def _():
                chain(wave, plane + distance, distance, 0).wait_recv()
                if distance < planes - 1:
                    send(wave, plane + distance, distance, 0)

            @pl.when(plane >= distance)
            def _():
                chain(wave, plane - distance, distance, 1).wait_recv()
                if distance < planes - 1:
                    send(wave, plane - distance, distance, 1)

        wave = tick - planes + 1
        if 0 <= wave < waves:
            stage(wave)
            for step in range(mates):
                pick(wave, step).start()

    for wave in range(waves):
        for step in range(1, mates):
            spread(wave, step).wait_send()
        for distance in range(planes - 1):

            @pl.when((plane + distance < planes) & has_left)
            def _():
                chain(wave, plane + distance, distance, 0).wait_send()

            @pl.when((plane >= distance) & has_right)
            def _():
                chain(wave, plane - distance, distance, 1).wait_send()

        pick(wave, 0).wait()
        for step in range(1, mates):
            pick(wave, step).wait()


def exchange(kq_map, wannier, count_x, count_y):
    rows_x, cols_y, bands, width = wannier.shape
    qpoints = kq_map.shape[0]
    planes, mates = count_y // CORES, count_x * CORES
    parts = mates // cols_y
    assert parts * cols_y == mates and planes * CORES == count_y
    waves = bands // (parts * SLAB)
    plan = (count_x, planes, rows_x, cols_y, qpoints, parts, waves)
    dma = pltpu.SemaphoreType.DMA
    return pl.pallas_call(
        functools.partial(exchange_kernel, plan),
        out_shape=jax.ShapeDtypeStruct((cols_y, qpoints, rows_x, bands, width), wannier.dtype),
        grid=(1,),
        in_specs=[
            pl.BlockSpec((qpoints, 128), lambda i: (0, 0), memory_space=pltpu.SMEM),
            pl.BlockSpec(memory_space=pl.ANY),
        ],
        out_specs=pl.BlockSpec(memory_space=pl.ANY),
        scratch_shapes=[pltpu.VMEM((count_y, count_x * rows_x, SLAB, width), wannier.dtype)] * waves
        + [pltpu.VMEM((mates, qpoints, rows_x, SLAB, width), wannier.dtype)] * waves
        + [
            dma((waves, mates)),
            dma((waves, mates)),
            dma((waves,)),
            dma((waves, planes, 2)),
            dma((waves, planes)),
            dma((waves, mates)),
            dma((waves, mates)),
            dma((waves,)),
        ],
        compiler_params=pltpu.CompilerParams(collective_id=0, has_side_effects=True),
    )(kq_map, wannier)


def rotate_kernel(column_ref, coupling_ref, wannier_ref, *refs):
    partner_refs, out_ref = refs[:-1], refs[-1]
    qpoints, rows, _, modes, bands, width = coupling_ref.shape
    half = width // 2
    for first in range(0, rows, 2):
        turned = []
        for row in (first, first + 1):
            real, imag = wannier_ref[row, 0, :, :half], wannier_ref[row, 0, :, half:]
            factor = jnp.concatenate(
                [jnp.concatenate([real, imag], axis=1), jnp.concatenate([-imag, real], axis=1)], axis=0
            )
            blank = jnp.zeros_like(factor)
            pair_factor = jnp.concatenate(
                [jnp.concatenate([factor, blank], axis=1), jnp.concatenate([blank, factor], axis=1)], axis=0
            )
            blocks = coupling_ref[:, row, 0].reshape(qpoints * modes // 2, 2, bands, width)
            pairs = jnp.concatenate([blocks[:, 0].reshape(-1, width), blocks[:, 1].reshape(-1, width)], axis=1)
            turned.append(jnp.dot(pairs, pair_factor, preferred_element_type=jnp.float32).astype(jnp.bfloat16))
        for q in range(qpoints):
            stacked, partner_rows = [], []
            for side, row in enumerate((first, first + 1)):
                parts = []
                for mode in range(modes):
                    pair, lane = divmod(q * modes + mode, 2)
                    own = turned[side][pair * bands : (pair + 1) * bands, lane * width : (lane + 1) * width]
                    swapped = jnp.concatenate([own[:, half:], -own[:, :half]], axis=1)
                    parts.append(jnp.concatenate([own, swapped], axis=0))
                stacked.append(jnp.concatenate(parts, axis=1))
                partner = partner_refs[q][0, 0, row]
                column = jnp.concatenate([partner[:, :half], partner[:, half:]], axis=0)
                blank = jnp.zeros_like(column)
                partner_rows.append(jnp.concatenate([blank, column] if side else [column, blank], axis=1))
            rotated = lax.dot_general(
                jnp.concatenate(partner_rows, axis=0),
                jnp.concatenate(stacked, axis=0),
                (((0,), (0,)), ((), ())),
                preferred_element_type=jnp.float32,
            ).astype(jnp.bfloat16)
            for side, row in enumerate((first, first + 1)):
                for mode in range(modes):
                    out_ref[q, row, 0, mode] = rotated[side * bands : (side + 1) * bands, mode * width : (mode + 1) * width]


def rotate(columns, coupling, wannier, partner):
    qpoints, rows, cols, modes, bands, width = coupling.shape
    all_modes = pl.BlockSpec((qpoints, rows, 1, modes, bands, width), lambda p, c: (0, 0, p, 0, 0, 0))

    def partner_spec(q):
        return pl.BlockSpec((1, 1, rows, bands, width), lambda p, c: ((p + c[q]) % cols, q, 0, 0, 0))

    return pl.pallas_call(
        rotate_kernel,
        grid_spec=pltpu.PrefetchScalarGridSpec(
            num_scalar_prefetch=1,
            grid=(cols,),
            in_specs=[all_modes, pl.BlockSpec((rows, 1, bands, width), lambda p, c: (0, p, 0, 0))]
            + [partner_spec(q) for q in range(qpoints)],
            out_specs=all_modes,
        ),
        out_shape=jax.ShapeDtypeStruct(coupling.shape, coupling.dtype),
    )(columns, coupling, wannier, *[partner] * qpoints)


def per_device(wannier, coupling, kq_map):
    count_x, count_y = lax.axis_size("kx"), lax.axis_size("ky")
    partner = exchange(kq_map, wannier, count_x, count_y)
    return rotate(kq_map[:, 0] % wannier.shape[1], coupling, wannier, partner)


def solution(mesh):
    in_specs = (P("kx", "ky", None, None), P(None, "kx", "ky", None, None, None), P())
    out_specs = P(None, "kx", "ky", None, None, None)
    return jax.shard_map(
        per_device, mesh=mesh, in_specs=in_specs, out_specs=out_specs, check_vma=False
    )
```

time: 109 us -> 72.1 us (0.66); the launches traced: 111 us -> 71.5 us
  waiting for transfers between devices: 67 us -> 0 us
  Pallas kernels: 14.7 us -> 70.2 us
  starting transfers between devices: 10.9 us -> 0 us
  between operations: 7.71 us -> 0.01 us
  local copies, waits for them, and re-layouts: 7.57 us -> 0.8 us
  other arithmetic: 2.55 us -> 0.55 us
    ppermute x10 -> x0, waiting for transfers between devices: 67 us -> none  [shift_blocks(): return lax.ppermute(block, ('kx', 'ky'), pairs)]
    pallas_call x1 -> x2, Pallas kernels: 14.7 us -> 70.2 us  [the longest x1 54.1 us: exchange(): pl.pallas_call(functools.partial(exchange_kernel, plan), out_shape=jax.Sh...]
    ppermute x10 -> x0, starting transfers between devices: 10.9 us -> none  [shift_blocks(): return lax.ppermute(block, ('kx', 'ky'), pairs)]
    slice x6 -> x1, local copies, waits for them, and re-layouts: 6.27 us -> 0.8 us  [per_device(): return rotate(kq_map[:, 0] % wannier.shape[1], coupling, wannier, partner)]
    concatenate x3 -> x0, other arithmetic: 2.55 us -> none  [shift_rows(): return jnp.concatenate([near, far], axis=0)]
  transfers between devices with their start and end apart: 10 -> 0, of which waited for: 7 -> 0; matrix products, arithmetic and copies ran while one was open for 4% -> 0% of each run, Pallas kernels for 0% -> 0%
where the time goes in v1:
time: 72.1 us; the launch traced here: 71.5 us
  Pallas kernels  70.2 us (97%)
  local copies, waits for them, and re-layouts  0.8 us (1%)
    pallas_call x1, Pallas kernels, exchange(): pl.pallas_call(functools.partial(exchange_kernel, plan), out_shape=jax.Sh...  54.1 us
    pallas_call x1, Pallas kernels, rotate(): pl.pallas_call(rotate_kernel, grid_spec=pltpu.PrefetchScalarGridSpec(num_...  16 us

profile of v1, /device:TPU:0, one launch (start us, length us, event | category | flops | bytes accessed | tf_op | source)
XLA Modules:
  0.0 71.5 jit_solution(9889915998586482458)
XLA Ops:
  0.0 0.8 %slice_reduce_fusion = s32[3]{0:T(128)S(1)} fusion(s32[3,1024]{1,0:T(4,128)} %map_ref.1), kind=kLoop, calls=%fused_computation.2 | loop fusion | bytes 24 | tf_op jit(solution)/shard_map/slice | solution.py:248
  0.8 0.6 and_select_fusion.column_ref
  1.3 54.1 %shard_map.37.refs_0_.refs_1_.refs_2_ = bf16[8,3,4,64,128]{4,3,2,1,0:T(8,128)(2,1)} custom-call(s32[3,1024]{1,0:T(4,128)} %map_ref.1, bf16[4,8,64,128]{3,2,1,0:T(8,128)(2,1)} %wannier_ref.3), custom_call_target="tpu_custom_call" | custom-call | tf_op jit(solution)/shard_map/pallas_call | solution.py:157
  55.5 16.0 %shard_map.38 = bf16[3,4,8,6,64,128]{5,4,3,2,1,0:T(8,128)(2,1)} custom-call(s32[3]{0:T(128)} %and_select_fusion.column_ref, bf16[3,4,8,6,64,128]{5,4,3,2,1,0:T(8,128)(2,1)} %coupling_ref.1, bf16[4,8,64,128]{3,2,1,0:T(8,128)(2,1)} %wannier_ref.3, bf16[8,3,4,64,128]{4,3,2,1,0:T(8,128)(2,1)} %shard_map.37.refs_0_.refs_1_.refs_2_, ...), custom_call_target="tpu_custom_call" | custom-call | tf_op jit(solution)/shard_map/pallas_call | solution.py:232

commit v2 on v1

v2 whole, which is shorter than its diff:
```python
import functools

import jax
import jax.numpy as jnp
from jax import lax
from jax.experimental import pallas as pl
from jax.experimental.pallas import tpu as pltpu
from jax.sharding import PartitionSpec as P

MESH = pl.DeviceIdType.MESH
CORES = 2
SLAB = 16
UNROLL = 8
DEPTH = 4


def turn_point(coupling, wannier, out):
    qpoints, modes, bands, width = coupling.shape
    half = width // 2
    real, imag = wannier[:, :half], wannier[:, half:]
    plain = jnp.concatenate([jnp.concatenate([real, imag], axis=1), jnp.concatenate([-imag, real], axis=1)], axis=0)
    swapped = jnp.concatenate([jnp.concatenate([imag, -real], axis=1), jnp.concatenate([real, imag], axis=1)], axis=0)
    blank = jnp.zeros_like(plain)
    blocks = coupling[...].reshape(qpoints * modes // 2, 2, bands, width)
    pairs = jnp.concatenate([blocks[:, 0].reshape(-1, width), blocks[:, 1].reshape(-1, width)], axis=1)
    for side, factor in enumerate((plain, swapped)):
        pair_factor = jnp.concatenate(
            [jnp.concatenate([factor, blank], axis=1), jnp.concatenate([blank, factor], axis=1)], axis=0
        )
        turned = jnp.dot(pairs, pair_factor, preferred_element_type=jnp.float32).astype(out.dtype)
        for index in range(qpoints * modes):
            pair, lane = divmod(index, 2)
            q, mode = divmod(index, modes)
            out[q, side * bands : (side + 1) * bands, mode * width : (mode + 1) * width] = turned[
                pair * bands : (pair + 1) * bands, lane * width : (lane + 1) * width
            ]


def exchange_kernel(plan, map_hbm, wannier_hbm, coupling_ref, partner_ref, turned_ref, *scratch):
    count_x, planes, rows_x, cols_y, qpoints, parts, waves = plan
    mates = count_x * CORES
    total_x, total_y, blocks = count_x * rows_x, planes * CORES * cols_y, planes * CORES
    gathered, staged, arrived = (scratch[part * waves : (part + 1) * waves] for part in range(3))
    spread_send, spread_recv, spread_self, chain_send, chain_recv, pick_send, pick_recv = scratch[3 * waves :][:7]
    map_ref, map_sem, wannier_ref, wannier_sem, held_in, in_sem = scratch[3 * waves + 7 :]
    points, depth = rows_x * cols_y, held_in.shape[0]

    here_x, here_y = lax.axis_index("kx"), lax.axis_index("ky")
    plane, core = here_y // CORES, here_y % CORES
    mate = here_x * CORES + core

    def device_of(other):
        return (other // CORES, plane * CORES + other % CORES)

    def part_of(other):
        return other // cols_y if parts > 1 else 0

    def slab(part, wave):
        return pl.ds(pl.multiple_of((part * waves + wave) * SLAB, SLAB), SLAB)

    def spread(wave, step):
        other = (mate + step) % mates
        window = (slice(None), other % cols_y, slab(part_of(other), wave), slice(None))
        target = gathered[wave].at[here_y, pl.ds(here_x * rows_x, rows_x)]
        if step == 0:
            return pltpu.make_async_copy(wannier_hbm.at[window], target, spread_self.at[wave])
        source = wannier_ref.at[window]
        return pltpu.make_async_remote_copy(
            source, target, spread_send.at[wave, step], spread_recv.at[wave, step], device_of(other), MESH
        )

    def chain(wave, origin, distance, side):
        block = gathered[wave].at[pl.ds(origin * CORES, CORES)]
        target = (here_x, here_y + (CORES if side else -CORES))
        return pltpu.make_async_remote_copy(
            block, block, chain_send.at[wave, distance, side], chain_recv.at[wave, origin], target, MESH
        )

    def pick(wave, step):
        source = staged[wave].at[step]
        target = arrived[wave].at[mate]
        return pltpu.make_async_remote_copy(
            source, target, pick_send.at[wave, step], pick_recv.at[wave, step], device_of((mate + step) % mates), MESH
        )

    def stage(wave):
        kind = mate % cols_y

        def one(step, carry):
            other = (mate + step) % mates
            for q in range(qpoints):
                shift_x, shift_y = map_ref[q, 0] // total_y, map_ref[q, 0] % total_y
                block = (plane * CORES + other % CORES + (shift_y - kind + cols_y - 1) // cols_y) % blocks
                for row in range(rows_x):
                    staged[wave][step, q, row] = gathered[wave][block, (other // CORES * rows_x + shift_x + row) % total_x]
            return carry

        lax.fori_loop(0, mates, one, 0)
        for q in range(qpoints):
            for row in range(rows_x):
                arrived[wave][mate, q, row] = staged[wave][0, q, row]

    def settle(wave):
        for step in range(1, mates):
            pick(wave, step).wait_recv()

        def one(col, carry):
            for q in range(qpoints):
                for part in range(parts):
                    source = part * cols_y + (col + map_ref[q, 0]) % cols_y
                    for row in range(rows_x):
                        partner_ref[col, q, row, slab(part, wave), :] = arrived[wave][source, q, row]
            return carry

        lax.fori_loop(0, cols_y, one, 0)

    def fetch(point):
        slot = point % depth
        return pltpu.make_async_copy(coupling_ref.at[:, point % rows_x, point // rows_x], held_in.at[slot], in_sem.at[slot])

    def turn(point, carry):
        slot = point % depth
        fetch(point).wait()
        turn_point(held_in.at[slot], wannier_ref[point % rows_x, point // rows_x], turned_ref.at[point // rows_x, point % rows_x])

        @pl.when(point + depth < points)
        def _():
            fetch(point + depth).start()

        return carry

    turned = 0

    def fill(count):
        nonlocal turned
        last = min(points, turned + count)
        if last > turned:
            lax.fori_loop(turned, last, turn, 0)
        turned = last

    map_copy = pltpu.make_async_copy(map_hbm, map_ref, map_sem)
    wannier_copy = pltpu.make_async_copy(wannier_hbm, wannier_ref, wannier_sem)
    wannier_copy.start()
    map_copy.start()
    for point in range(depth):
        fetch(point).start()

    has_left, has_right = plane > 0, plane < planes - 1

    barrier = pltpu.get_barrier_semaphore()
    for step in range(1, mates):
        pl.semaphore_signal(barrier, inc=1, device_id=device_of((mate + step) % mates), device_id_type=MESH)

    @pl.when(has_left)
    def _():
        pl.semaphore_signal(barrier, inc=1, device_id=(here_x, here_y - CORES), device_id_type=MESH)

    @pl.when(has_right)
    def _():
        pl.semaphore_signal(barrier, inc=1, device_id=(here_x, here_y + CORES), device_id_type=MESH)

    pl.semaphore_wait(barrier, mates - 1 + has_left.astype(jnp.int32) + has_right.astype(jnp.int32))

    wannier_copy.wait()
    for wave in range(waves):
        for step in range(mates):
            spread(wave, step).start()
    map_copy.wait()

    def send(wave, origin, distance, side):
        @pl.when(has_right if side else has_left)
        def _():
            chain(wave, origin, distance, side).start()

    def launch(wave):
        spread(wave, 0).wait()
        for step in range(1, mates):
            spread(wave, step).wait_recv()
        for side in range(2):
            send(wave, plane, 0, side)

    for wave in range(min(2, waves)):
        fill(2)
        launch(wave)

    for tick in range(1, waves + planes - 1):
        for distance in reversed(range(1, planes)):
            wave = tick - distance
            if not 0 <= wave < waves:
                continue
            fill(2)

            @pl.when(plane + distance < planes)
            def _():
                chain(wave, plane + distance, distance, 0).wait_recv()
                if distance < planes - 1:
                    send(wave, plane + distance, distance, 0)

            @pl.when(plane >= distance)
            def _():
                chain(wave, plane - distance, distance, 1).wait_recv()
                if distance < planes - 1:
                    send(wave, plane - distance, distance, 1)

        if tick + 1 < waves:
            launch(tick + 1)
        wave = tick - planes + 1
        if 0 <= wave < waves:
            stage(wave)
            for step in range(1, mates):
                pick(wave, step).start()
            if wave > 0:
                settle(wave - 1)

    fill(points)
    settle(waves - 1)

    for wave in range(waves):
        for step in range(1, mates):
            spread(wave, step).wait_send()
        for distance in range(planes - 1):

            @pl.when((plane + distance < planes) & has_left)
            def _():
                chain(wave, plane + distance, distance, 0).wait_send()

            @pl.when((plane >= distance) & has_right)
            def _():
                chain(wave, plane - distance, distance, 1).wait_send()

        for step in range(1, mates):
            pick(wave, step).wait_send()


def exchange(kq_map, wannier, coupling, count_x, count_y):
    rows_x, cols_y, bands, width = wannier.shape
    qpoints, modes = coupling.shape[0], coupling.shape[3]
    planes, mates = count_y // CORES, count_x * CORES
    parts = mates // cols_y
    assert parts * cols_y == mates and planes * CORES == count_y
    waves = bands // (parts * SLAB)
    plan = (count_x, planes, rows_x, cols_y, qpoints, parts, waves)
    dma = pltpu.SemaphoreType.DMA
    hbm, vmem = pl.BlockSpec(memory_space=pltpu.HBM), pl.BlockSpec(memory_space=pltpu.VMEM)
    kind = coupling.dtype
    return pl.pallas_call(
        functools.partial(exchange_kernel, plan),
        out_shape=[
            jax.ShapeDtypeStruct((cols_y, qpoints, rows_x, bands, width), kind),
            jax.ShapeDtypeStruct((cols_y, rows_x, qpoints, 2 * bands, modes * width), kind),
        ],
        in_specs=[hbm, hbm, hbm],
        out_specs=[vmem, vmem],
        scratch_shapes=[pltpu.VMEM((count_y, count_x * rows_x, SLAB, width), kind)] * waves
        + [pltpu.VMEM((mates, qpoints, rows_x, SLAB, width), kind)] * (2 * waves)
        + [
            dma((waves, mates)),
            dma((waves, mates)),
            dma((waves,)),
            dma((waves, planes, 2)),
            dma((waves, planes)),
            dma((waves, mates)),
            dma((waves, mates)),
            pltpu.SMEM(kq_map.shape, jnp.int32),
            dma(()),
            pltpu.VMEM(wannier.shape, kind),
            dma(()),
            pltpu.VMEM((DEPTH, qpoints, modes, bands, width), kind),
            dma((DEPTH,)),
        ],
        compiler_params=pltpu.CompilerParams(collective_id=0, has_side_effects=True, vmem_limit_bytes=16 << 20),
    )(*[pltpu.with_memory_space_constraint(a, pltpu.HBM) for a in (kq_map, wannier, coupling)])


def rotate_kernel(partner_ref, turned_ref, out_hbm, out_ref, out_sem):
    cols, qpoints, rows, modes, bands, width = out_ref.shape
    half = width // 2

    def flush(col):
        return pltpu.make_async_copy(out_ref.at[col], out_hbm.at[:, :, col], out_sem.at[col])

    def one(col, carry):
        for q in range(qpoints):
            for first in range(0, rows, 2):
                partner_rows = []
                for side, row in enumerate((first, first + 1)):
                    partner = partner_ref[col, q, row]
                    column = jnp.concatenate([partner[:, :half], partner[:, half:]], axis=0)
                    blank = jnp.zeros_like(column)
                    partner_rows.append(jnp.concatenate([blank, column] if side else [column, blank], axis=1))
                rotated = lax.dot_general(
                    jnp.concatenate(partner_rows, axis=0),
                    jnp.concatenate([turned_ref[col, row, q] for row in (first, first + 1)], axis=0),
                    (((0,), (0,)), ((), ())),
                    preferred_element_type=jnp.float32,
                ).astype(out_ref.dtype)
                for side, row in enumerate((first, first + 1)):
                    for mode in range(modes):
                        out_ref[col, q, row, mode] = rotated[side * bands : (side + 1) * bands, mode * width : (mode + 1) * width]
        flush(col).start()
        return carry

    lax.fori_loop(0, cols, one, 0, unroll=UNROLL)
    for col in range(cols):
        flush(col).wait()


def rotate(turned, partner):
    cols, qpoints, rows, bands, width = partner.shape
    modes = turned.shape[-1] // width
    hbm, vmem = pl.BlockSpec(memory_space=pltpu.HBM), pl.BlockSpec(memory_space=pltpu.VMEM)
    return pl.pallas_call(
        rotate_kernel,
        in_specs=[vmem, vmem],
        out_specs=hbm,
        out_shape=jax.ShapeDtypeStruct((qpoints, rows, cols, modes, bands, width), turned.dtype),
        scratch_shapes=[
            pltpu.VMEM((cols, qpoints, rows, modes, bands, width), turned.dtype),
            pltpu.SemaphoreType.DMA((cols,)),
        ],
        compiler_params=pltpu.CompilerParams(vmem_limit_bytes=16 << 20),
    )(partner, turned)


def per_device(wannier, coupling, kq_map):
    partner, turned = exchange(kq_map, wannier, coupling, lax.axis_size("kx"), lax.axis_size("ky"))
    return rotate(turned, partner)


def solution(mesh):
    in_specs = (P("kx", "ky", None, None), P(None, "kx", "ky", None, None, None), P())
    out_specs = P(None, "kx", "ky", None, None, None)
    return jax.shard_map(
        per_device, mesh=mesh, in_specs=in_specs, out_specs=out_specs, check_vma=False
    )
```

time: 72.1 us -> 59.3 us (0.82)
  Pallas kernels: 70.2 us -> 59.1 us
  local copies, waits for them, and re-layouts: 0.8 us -> 0 us
    pallas_call x2, Pallas kernels: 70.2 us -> 59.1 us  [the longest x1 53.2 us: exchange(): pl.pallas_call(functools.partial(exchange_kernel, plan), out_shape=[jax.S...]
    slice x1 -> x0, local copies, waits for them, and re-layouts: 0.8 us -> none  [per_device(): return rotate(kq_map[:, 0] % wannier.shape[1], coupling, wannier, partner)]
where the time goes in v2:
time: 59.3 us; the launch traced here: 59.1 us
  Pallas kernels  59.1 us (100%)
    pallas_call x1, Pallas kernels, exchange(): pl.pallas_call(functools.partial(exchange_kernel, plan), out_shape=[jax.S...  53.2 us
    pallas_call x1, Pallas kernels, rotate(): pl.pallas_call(rotate_kernel, in_specs=[vmem, vmem], out_specs=hbm, out_s...  5.96 us

profile of v2, /device:TPU:0, one launch (start us, length us, event | category | flops | bytes accessed | tf_op | source)
XLA Modules:
  0.0 59.1 jit_solution(1646273201931944053)
XLA Ops:
  0.0 53.2 %shard_map.37 = (bf16[8,3,4,64,128]{4,3,2,1,0:T(8,128)(2,1)S(1)}, bf16[8,4,3,128,768]{4,3,2,1,0:T(8,128)(2,1)S(1)}) custom-call(s32[3,1024]{1,0:T(4,128)} %map_hbm.1, bf16[4,8,64,128]{3,2,1,0:T(8,128)(2,1)} %wannier_hbm.1, bf16[3,4,8,6,64,128]{5,4,3,2,1,0:T(8,128)(2,1)} %coupling_ref.1), custom_call_target="tpu_custom_call" | custom-call | tf_op jit(solution)/shard_map/pallas_call | solution.py:246
  53.2 6.0 %shard_map.38 = bf16[3,4,8,6,64,128]{5,4,3,2,1,0:T(8,128)(2,1)} custom-call(bf16[8,3,4,64,128]{4,3,2,1,0:T(8,128)(2,1)S(1)} %get-tuple-element.7.partner_ref, bf16[8,4,3,128,768]{4,3,2,1,0:T(8,128)(2,1)S(1)} %get-tuple-element.8.turned_ref), custom_call_target="tpu_custom_call" | custom-call | tf_op jit(solution)/shard_map/pallas_call | solution.py:312
